TPU v7x, 32 devices: a whole 2x2x4 slice. The times are simulated.
32 devices in a mesh: fsdp: 4 (over y, x), ep: 8 (over z, core).
Axes of the slice: x: 2, y: 2, z: 4, core: 2. Of those that a mesh axis runs over, the one named last changes fastest.
Arguments:
- hidden_in: bfloat16 [8192, 2048], P(('fsdp', 'ep')), may hold values from -6 to 6
- norm_gain: float32 [2048], replicated, may hold values from 0.25 to 1.75
- expert_ids: int32 [8192, 8], P(('fsdp', 'ep')), may hold values from 0 to 15, all different within a row; in each aligned block of 256 rows (0 to 255, 256 to 511, ...) at most 160 rows name the same one
- expert_probs: float32 [8192, 8], P(('fsdp', 'ep')), may hold values from 0.05 to 0.25
- gate_proj: bfloat16 [16, 2048, 768], P('ep', 'fsdp'), may hold values from -0.125 to 0.125
- up_proj: bfloat16 [16, 2048, 768], P('ep', 'fsdp'), may hold values from -0.125 to 0.125
- down_proj: bfloat16 [16, 768, 2048], P('ep', None, 'fsdp'), may hold values from -0.21875 to 0.21875
Outputs:
- moe_out: bfloat16 [8192, 2048], P(('fsdp', 'ep'))
Inputs may be any that keep to these rules, and one draw needn't show every extreme that they name: `expert_ids`: within the rows of one device (aligned blocks of 256 rows) each expert id is named by at most 160 rows, and in some blocks one expert by exactly 160; the 8 ids of a row are distinct.
All inputs are finite; a program needn't handle non-finite values.
Results may differ from a plain program's by a relative error of at most 0.0025.
Values may be sent and summed in bfloat16 or wider, within the bound.
A program may use at most 128 MiB of HBM per device.

v0:
```python
import jax
import jax.numpy as jnp
from jax import lax
from jax.sharding import PartitionSpec as P


def rms_norm(hidden_in, norm_gain):
    values = hidden_in.astype(jnp.float32)
    spread = jnp.mean(values * values, axis=-1, keepdims=True)
    return (values * lax.rsqrt(spread + 1e-06) * norm_gain).astype(jnp.bfloat16)


def per_device(hidden_in, norm_gain, expert_ids, expert_probs, gate_proj, up_proj, down_proj):
    local_experts = gate_proj.shape[0]
    normed = rms_norm(hidden_in, norm_gain)
    all_experts = local_experts * lax.axis_size("ep")
    hot = expert_ids[:, :, None] == jnp.arange(all_experts, dtype=jnp.int32)
    weights = jnp.sum(jnp.where(hot, expert_probs[:, :, None], 0.0), axis=1)
    tokens = lax.all_gather(normed, "ep", axis=0, tiled=True)
    routed = lax.all_to_all(
        weights.reshape(weights.shape[0], lax.axis_size("ep"), local_experts),
        "ep",
        split_axis=1,
        concat_axis=0,
        tiled=True,
    ).reshape(tokens.shape[0], local_experts)
    total = 0.0
    gate_all = lax.all_gather(gate_proj, "fsdp", axis=1, tiled=True)
    up_all = lax.all_gather(up_proj, "fsdp", axis=1, tiled=True)
    down_all = lax.all_gather(down_proj, "fsdp", axis=2, tiled=True)
    for e in range(local_experts):
        gate = jnp.dot(tokens, gate_all[e], preferred_element_type=jnp.float32)
        up = jnp.dot(tokens, up_all[e], preferred_element_type=jnp.float32)
        act = (jax.nn.silu(gate) * up).astype(jnp.bfloat16)
        out = jnp.dot(act, down_all[e], preferred_element_type=jnp.float32).astype(jnp.bfloat16)
        total = total + out.astype(jnp.float32) * routed[:, e, None]
    combined = lax.psum_scatter(total, "ep", scatter_dimension=0, tiled=True)
    return combined.astype(jnp.bfloat16)


def solution(mesh):
    return jax.shard_map(
        per_device,
        mesh=mesh,
        in_specs=(
            P(("fsdp", "ep"), None),
            P(),
            P(("fsdp", "ep"), None),
            P(("fsdp", "ep"), None),
            P("ep", "fsdp", None),
            P("ep", "fsdp", None),
            P("ep", None, "fsdp"),
        ),
        out_specs=P(("fsdp", "ep"), None),
        check_vma=False,
    )
```

profile of v0, /device:TPU:0, one launch (start us, length us, event | category | flops | bytes accessed | tf_op | source)
XLA Modules:
  0.0 533.1 jit_solution(4729882364466384271)
XLA Ops:
  6.5 0.0 copy-start
  6.5 0.0 copy-start.1
  6.5 0.0 all-gather.7.cloned.1.call-start
  6.5 0.7 all-gather.7.cloned.1.call-update
  7.3 0.0 all-gather.5.cloned.1.call-start
  7.3 1.5 fusion.5
  8.8 2.5 fusion.7
  11.3 0.0 all-gather.5.cloned.1.call-update
  11.4 0.0 all-gather.9.cloned.1.call-start
  11.4 0.7 all-gather.9.cloned.1.call-update
  12.1 0.0 all-gather.11.cloned.1.call-start
  12.1 0.5 all-gather.11.cloned.1.call-update
  12.7 0.0 reduce-scatter.2.cloned.1.call-start
  12.7 0.0 copy-done
  12.7 0.0 copy-done.1
  12.8 11.8 %all_to_all.15 = f32[256,8,2]{0,2,1:T(2,128)S(1)} all-to-all(f32[256,8,2]{0,2,1:T(2,128)S(1)} %reshape.18), channel_id=1, replica_groups=mesh['fsdp'=4,'ep'=8] {'ep'}, dimensions={1} | all-to-all | bytes 32768 | tf_op jit(solution)/shard_map/all_to_all | solution.py:20
  24.6 57.4 %all-gather.7.cloned.1.call-done = bf16[2,2048,768]{2,1,0:T(8,128)(2,1)} async-done(((bf16[2,512,768]{2,1,0:T(8,128)(2,1)}), bf16[2,2048,768]{2,1,0:T(8,128)(2,1)}) %all-gather.7.cloned.1.call-update) | async-done | bytes 6291472 | tf_op jit(solution)/shard_map/all_gather | solution.py:28
  82.0 83.7 %all-gather.5.cloned.1.call-done = bf16[2048,2048]{1,0:T(8,128)(2,1)} async-done(((bf16[256,2048]{1,0:T(8,128)(2,1)}), bf16[2048,2048]{1,0:T(8,128)(2,1)}) %all-gather.5.cloned.1.call-update) | async-done | bytes 8388624 | tf_op jit(solution)/shard_map/all_gather | solution.py:19
  165.6 0.0 copy-start.2
  165.6 0.0 copy-start.3
  165.6 11.8 %fusion.1 = f32[2048,768]{1,0:T(8,128)} fusion(bf16[2048,2048]{1,0:T(8,128)(2,1)} %all-gather.5.cloned.1.call-done, bf16[2,2048,768]{2,1,0:T(8,128)(2,1)} %all-gather.7.cloned.1.call-done), kind=kOutput, calls=%fused_computation.7 | convolution fusion | flops 6442450944 | bytes 17825792 | tf_op jit(solution)/shard_map/dot_general | solution.py:32
  177.4 0.0 copy-done.2
  177.4 0.0 copy-done.3
  177.4 8.5 %fusion.2 = f32[2048,768]{1,0:T(8,128)} fusion(bf16[2048,2048]{1,0:T(8,128)(2,1)S(1)} %copy-done.2, bf16[2,2048,768]{2,1,0:T(8,128)(2,1)S(1)} %copy-done.3), kind=kOutput, calls=%fused_computation.11 | convolution fusion | flops 6442450944 | bytes 17825792 | tf_op jit(solution)/shard_map/dot_general | solution.py:32
  185.9 50.1 %all-gather.9.cloned.1.call-done = bf16[2,2048,768]{2,1,0:T(8,128)(2,1)} async-done(((bf16[2,512,768]{2,1,0:T(8,128)(2,1)}), bf16[2,2048,768]{2,1,0:T(8,128)(2,1)}) %all-gather.9.cloned.1.call-update) | async-done | bytes 6291472 | tf_op jit(solution)/shard_map/all_gather | solution.py:29
  236.0 71.6 %all-gather.11.cloned.1.call-done = bf16[2,768,2048]{2,1,0:T(8,128)(2,1)} async-done(((bf16[2,768,512]{2,1,0:T(8,128)(2,1)}), bf16[2,768,2048]{2,1,0:T(8,128)(2,1)}) %all-gather.11.cloned.1.call-update) | async-done | bytes 6291472 | tf_op jit(solution)/shard_map/all_gather | solution.py:30
  307.6 22.1 %fusion = bf16[2048,2048]{1,0:T(8,128)(2,1)} fusion(f32[2048,768]{1,0:T(8,128)} %fusion.2, bf16[2048,2048]{1,0:T(8,128)(2,1)} %all-gather.5.cloned.1.call-done, bf16[2,768,2048]{2,1,0:T(8,128)(2,1)} %all-gather.11.cloned.1.call-done, bf16[2,2048,768]{2,1,0:T(8,128)(2,1)} %all-gather.9.cloned.1.call-done), kind=kOutput, calls=%fused_computation.3 | convolution fusion | flops 12894339072 | bytes 29360128 | tf_op jit(solution)/shard_map/dot_general | solution.py:35
  329.7 25.8 %multiply_add_fusion = f32[2048,2048]{1,0:T(8,128)} fusion(f32[2048]{0:T(1024)S(1)} %bitcast.35, f32[2048]{0:T(1024)S(1)} %bitcast.34, bf16[2048,2048]{1,0:T(8,128)(2,1)} %fusion, f32[2048,768]{1,0:T(8,128)} %fusion.1, bf16[2048,2048]{1,0:T(8,128)(2,1)} %all-gather.5.cloned.1.call-done, bf16[2,768,2048]{2,1,0:T(8,128)(2,1)} %all-gather.11.cloned.1.call-done, ...), kind=kOutput, calls=%fused_computation | convolution fusion | flops 12919504896 | bytes 46153728 | tf_op jit(solution)/shard_map/dot_general | solution.py:35
  355.5 0.0 reduce-scatter.2.cloned.1.call-update
  355.5 168.3 %reduce-scatter.2.cloned.1.call-done = f32[256,2048]{1,0:T(8,128)} async-done(((f32[2048,2048]{1,0:T(8,128)}), f32[256,2048]{1,0:T(8,128)}) %reduce-scatter.2.cloned.1.call-update) | async-done | bytes 2097168 | tf_op jit(solution)/shard_map/reduce_scatter | solution.py:37
  523.8 2.7 convert_element_type.35
  (4 shorter events, 0.1 us)
Async XLA Ops:
  6.5 6.2 %copy-start = (f32[256,8]{0,1:T(8,128)S(1)}, f32[256,8]{0,1:T(8,128)}, u32[]{:S(2)}) copy-start(f32[256,8]{0,1:T(8,128)} %param.10) | copy-start | bytes 24580
  6.5 6.2 %copy-start.1 = (s32[256,8]{0,1:T(8,128)S(1)}, s32[256,8]{0,1:T(8,128)}, u32[]{:S(2)}) copy-start(s32[256,8]{0,1:T(8,128)} %param.9) | copy-start | bytes 24580
  6.5 75.4 %all-gather.7.cloned.1.call-start = ((), (), s32[]{:S(2)}) async-start(), calls=%async_computation.3 | async-start | bytes 7864320 | tf_op jit(solution)/shard_map/all_gather | solution.py:28
  7.3 158.4 %all-gather.5.cloned.1.call-start = ((), (), s32[]{:S(2)}) async-start(), calls=%async_computation.2 | async-start | bytes 9437184 | tf_op jit(solution)/shard_map/all_gather | solution.py:19
  11.4 224.7 %all-gather.9.cloned.1.call-start = ((), (), s32[]{:S(2)}) async-start(), calls=%async_computation.4 | async-start | bytes 7864320 | tf_op jit(solution)/shard_map/all_gather | solution.py:29
  12.1 295.5 %all-gather.11.cloned.1.call-start = ((), (), s32[]{:S(2)}) async-start(), calls=%async_computation.5 | async-start | bytes 7864320 | tf_op jit(solution)/shard_map/all_gather | solution.py:30
  12.7 511.2 %reduce-scatter.2.cloned.1.call-start = ((), (), s32[]{:S(2)}) async-start(), calls=%async_computation.6 | async-start | bytes 18874368 | tf_op jit(solution)/shard_map/reduce_scatter | solution.py:37
  165.6 11.8 %copy-start.2 = (bf16[2048,2048]{1,0:T(8,128)(2,1)S(1)}, bf16[2048,2048]{1,0:T(8,128)(2,1)}, u32[]{:S(2)}) copy-start(bf16[2048,2048]{1,0:T(8,128)(2,1)} %all-gather.5.cloned.1.call-done) | copy-start | bytes 25165828
  165.6 11.8 %copy-start.3 = (bf16[2,2048,768]{2,1,0:T(8,128)(2,1)S(1)}, bf16[2,2048,768]{2,1,0:T(8,128)(2,1)}, u32[]{:S(2)}) copy-start(bf16[2,2048,768]{2,1,0:T(8,128)(2,1)} %all-gather.7.cloned.1.call-done) | copy-start | bytes 18874372
Sparse Core Ops, SparseCore 0:
  9.2 72.7 all-gather.6
  83.6 82.0 all-gather.4
  167.5 68.5 all-gather.8
  237.7 69.8 all-gather.10
  355.6 168.1 reduce-scatter.1
where the time goes:
time: 533 us
  waiting for transfers between devices  433 us (81%)
  matrix products  68.2 us (13%)
  between operations  13.2 us (2%)
  blocking collectives  11.8 us (2%)
  other arithmetic  6.76 us (1%)
    reduce_scatter x1, waiting for transfers between devices, per_device(): combined = lax.psum_scatter(total, 'ep', scatter_dimension=0, tiled=True)  168 us
    all_gather x1, waiting for transfers between devices, per_device(): tokens = lax.all_gather(normed, 'ep', axis=0, tiled=True)  83.7 us
    all_gather x1, waiting for transfers between devices, per_device(): down_all = lax.all_gather(down_proj, 'fsdp', axis=2, tiled=True)  71.6 us
    all_gather x1, waiting for transfers between devices, per_device(): gate_all = lax.all_gather(gate_proj, 'fsdp', axis=1, tiled=True)  57.4 us
    all_gather x1, waiting for transfers between devices, per_device(): up_all = lax.all_gather(up_proj, 'fsdp', axis=1, tiled=True)  50.1 us
    dot_general x2, matrix products, per_device(): jnp.dot(act, down_all[e], preferred_element_type=jnp.float32)  47.9 us
    dot_general x2, matrix products, per_device(): gate = jnp.dot(tokens, gate_all[e], preferred_element_type=jnp.float32)  20.3 us
    all_to_all x1, blocking collectives, per_device(): lax.all_to_all(weights.reshape(weights.shape[0], lax.axis_size('ep'), loc...  11.8 us
  transfers between devices with their start and end apart: 5, of which 5 were waited for; matrix products, arithmetic and copies ran while one was open for 5% of the time, Pallas kernels for 0%

commit v1 on v0

--- a/solution.py
+++ b/solution.py
@@ -26,7 +26,12 @@
     ).reshape(tokens.shape[0], local_experts)
     total = 0.0
     gate_all = lax.all_gather(gate_proj, "fsdp", axis=1, tiled=True)
-    up_all = lax.all_gather(up_proj, "fsdp", axis=1, tiled=True)
+    ring = [up_proj]
+    for hop in range(3):
+        ring.append(lax.ppermute(ring[-1], "fsdp", [(dev, (dev + 1) % 4) for dev in range(4)]))
+    up_all = jnp.roll(
+        jnp.concatenate(ring[::-1], axis=1), (lax.axis_index("fsdp") + 1) * ring[0].shape[1], axis=1
+    )
     down_all = lax.all_gather(down_proj, "fsdp", axis=2, tiled=True)
     for e in range(local_experts):
         gate = jnp.dot(tokens, gate_all[e], preferred_element_type=jnp.float32)

time: 533 us -> 510 us (0.957)
  waiting for transfers between devices: 433 us -> 394 us
  local copies, waits for them, and re-layouts: 0.04 us -> 16.6 us
  blocking collectives: 11.8 us -> 0 us
  starting transfers between devices: 0.16 us -> 11.2 us
    ppermute x0 -> x3, waiting for transfers between devices: none -> 141 us  [per_device(): lax.ppermute(ring[-1], 'fsdp', [(dev, (dev + 1) % 4) for dev in range(4)])]
    all_gather x1, waiting for transfers between devices: 57.4 us -> 0.01 us  [per_device(): gate_all = lax.all_gather(gate_proj, 'fsdp', axis=1, tiled=True)]
    all_gather x1, waiting for transfers between devices: 83.7 us -> 27.4 us  [per_device(): tokens = lax.all_gather(normed, 'ep', axis=0, tiled=True)]
    all_gather x1 -> x0, waiting for transfers between devices: 50.1 us -> none  [per_device(): up_all = lax.all_gather(up_proj, 'fsdp', axis=1, tiled=True)]
    all_gather x1, waiting for transfers between devices: 71.6 us -> 49.9 us  [per_device(): down_all = lax.all_gather(down_proj, 'fsdp', axis=2, tiled=True)]
    unnamed x8 -> x17, local copies, waits for them, and re-layouts: 0.01 us -> 14.7 us
    all_to_all x1 -> x0, blocking collectives: 11.8 us -> none  [per_device(): lax.all_to_all(weights.reshape(weights.shape[0], lax.axis_size('ep'), loc...]
    all_to_all x0 -> x1, waiting for transfers between devices: none -> 7.01 us  [per_device(): lax.all_to_all(weights.reshape(weights.shape[0], lax.axis_size('ep'), loc...]
  transfers between devices with their start and end apart: 5 -> 8, of which waited for: 5 -> 7; matrix products, arithmetic and copies ran while one was open for 5% -> 8% of each run, Pallas kernels for 0% -> 0%
where the time goes in v1:
time: 510 us
  waiting for transfers between devices  394 us (77%)
  matrix products  68.2 us (13%)
  local copies, waits for them, and re-layouts  16.6 us (3%)
  between operations  13.2 us (3%)
  starting transfers between devices  11.2 us (2%)
  other arithmetic  6.76 us (1%)
    reduce_scatter x1, waiting for transfers between devices, per_device(): combined = lax.psum_scatter(total, 'ep', scatter_dimension=0, tiled=True)  168 us
    ppermute x3, waiting for transfers between devices, per_device(): lax.ppermute(ring[-1], 'fsdp', [(dev, (dev + 1) % 4) for dev in range(4)])  141 us
    all_gather x1, waiting for transfers between devices, per_device(): down_all = lax.all_gather(down_proj, 'fsdp', axis=2, tiled=True)  49.9 us
    dot_general x2, matrix products, per_device(): jnp.dot(act, down_all[e], preferred_element_type=jnp.float32)  47.9 us
    all_gather x1, waiting for transfers between devices, per_device(): tokens = lax.all_gather(normed, 'ep', axis=0, tiled=True)  27.4 us
    dot_general x2, matrix products, per_device(): gate = jnp.dot(tokens, gate_all[e], preferred_element_type=jnp.float32)  20.3 us
    unnamed x17, local copies, waits for them, and re-layouts  14.7 us
  transfers between devices with their start and end apart: 8, of which 7 were waited for; matrix products, arithmetic and copies ran while one was open for 8% of the time, Pallas kernels for 0%

profile of v1, /device:TPU:0, one launch (start us, length us, event | category | flops | bytes accessed | tf_op | source)
XLA Modules:
  0.0 509.8 jit_solution(5096666702530249026)
XLA Ops:
  6.5 0.0 copy-start.1
  6.5 0.0 copy-start.2
  6.5 0.0 all-gather.6.cloned.1.call-start
  6.5 0.7 all-gather.6.cloned.1.call-update
  7.3 0.0 all-gather.4.cloned.1.call-start
  7.3 1.5 fusion.5
  8.8 2.5 fusion.7
  11.3 0.0 copy-start
  11.3 0.0 all-gather.4.cloned.1.call-update
  11.4 0.0 all-gather.8.cloned.1.call-start
  11.4 3.0 collective-permute-start
  14.4 0.0 all-gather.8.cloned.1.call-update
  14.5 55.0 %collective-permute-done = bf16[2,512,768]{2,1,0:T(8,128)(2,1)S(1)} collective-permute-done((bf16[2,512,768]{2,1,0:T(8,128)(2,1)}, bf16[2,512,768]{2,1,0:T(8,128)(2,1)S(1)}, u32[]{:S(2)}, u32[]{:S(2)}) %collective-permute-start) | collective-permute-done | bytes 1572896 | tf_op jit(solution)/shard_map/ppermute | solution.py:31
  69.4 2.4 collective-permute-start.1
  71.8 62.6 %collective-permute-done.1 = bf16[2,512,768]{2,1,0:T(8,128)(2,1)} collective-permute-done((bf16[2,512,768]{2,1,0:T(8,128)(2,1)S(1)}, bf16[2,512,768]{2,1,0:T(8,128)(2,1)}, u32[]{:S(2)}, u32[]{:S(2)}) %collective-permute-start.1) | collective-permute-done | bytes 1572896 | tf_op jit(solution)/shard_map/ppermute | solution.py:31
  134.4 0.8 collective-permute-start.2
  135.1 0.0 copy-done.1
  135.1 0.0 copy-done.2
  135.2 0.6 reshape.18
  135.8 4.9 all-to-all-start
  140.7 0.0 reduce-scatter.2.cloned.1.call-start
  140.7 7.0 %all-to-all-done = f32[256,8,2]{0,2,1:T(2,128)S(1)} async-done(((f32[256,8,2]{0,2,1:T(2,128)}), f32[256,8,2]{0,2,1:T(2,128)S(1)}, u32[]{:S(2)}, u32[]{:S(2)}) %all-to-all-start) | async-done | bytes 16416 | tf_op jit(solution)/shard_map/all_to_all | solution.py:20
  147.8 23.0 %collective-permute-done.2 = bf16[2,512,768]{2,1,0:T(8,128)(2,1)} collective-permute-done((bf16[2,512,768]{2,1,0:T(8,128)(2,1)}, bf16[2,512,768]{2,1,0:T(8,128)(2,1)}, u32[]{:S(2)}, u32[]{:S(2)}) %collective-permute-start.2) | collective-permute-done | bytes 1572896 | tf_op jit(solution)/shard_map/ppermute | solution.py:31
  170.7 2.7 constant_dynamic-update-slice_fusion.7
  173.4 2.7 constant_dynamic-update-slice_fusion.6
  176.2 1.3 constant_dynamic-update-slice_fusion.5
  177.5 0.0 copy-done
  177.5 1.3 constant_dynamic-update-slice_fusion.4
  178.8 2.7 constant_dynamic-update-slice_fusion.3
  181.5 2.7 constant_dynamic-update-slice_fusion.2
  184.1 1.3 constant_dynamic-update-slice_fusion.1
  185.4 1.3 constant_dynamic-update-slice_fusion
  186.7 0.0 all-gather.6.cloned.1.call-done
  186.7 27.4 %all-gather.4.cloned.1.call-done = bf16[2048,2048]{1,0:T(8,128)(2,1)} async-done(((bf16[256,2048]{1,0:T(8,128)(2,1)}), bf16[2048,2048]{1,0:T(8,128)(2,1)}) %all-gather.4.cloned.1.call-update) | async-done | bytes 8388624 | tf_op jit(solution)/shard_map/all_gather | solution.py:19
  214.1 0.0 copy-start.3
  214.1 0.0 copy-start.4
  214.1 11.8 %fusion.1 = f32[2048,768]{1,0:T(8,128)} fusion(bf16[2048,2048]{1,0:T(8,128)(2,1)} %all-gather.4.cloned.1.call-done, bf16[2,2048,768]{2,1,0:T(8,128)(2,1)} %all-gather.6.cloned.1.call-done), kind=kOutput, calls=%fused_computation.7 | convolution fusion | flops 6442450944 | bytes 17825792 | tf_op jit(solution)/shard_map/dot_general | solution.py:37
  225.9 0.0 copy-done.3
  225.9 0.0 copy-done.4
  225.9 8.5 %fusion.2 = f32[2048,768]{1,0:T(8,128)} fusion(bf16[2048,2048]{1,0:T(8,128)(2,1)S(1)} %copy-done.3, bf16[2,2048,768]{2,1,0:T(8,128)(2,1)S(1)} %copy-done.4), kind=kOutput, calls=%fused_computation.11 | convolution fusion | flops 6442450944 | bytes 17825792 | tf_op jit(solution)/shard_map/dot_general | solution.py:37
  234.4 49.9 %all-gather.8.cloned.1.call-done = bf16[2,768,2048]{2,1,0:T(8,128)(2,1)} async-done(((bf16[2,768,512]{2,1,0:T(8,128)(2,1)}), bf16[2,768,2048]{2,1,0:T(8,128)(2,1)}) %all-gather.8.cloned.1.call-update) | async-done | bytes 6291472 | tf_op jit(solution)/shard_map/all_gather | solution.py:35
  284.3 22.1 %fusion = bf16[2048,2048]{1,0:T(8,128)(2,1)} fusion(f32[2048,768]{1,0:T(8,128)} %fusion.2, bf16[2048,2048]{1,0:T(8,128)(2,1)} %all-gather.4.cloned.1.call-done, bf16[2,768,2048]{2,1,0:T(8,128)(2,1)} %all-gather.8.cloned.1.call-done, bf16[2,4096,768]{2,1,0:T(8,128)(2,1)} %constant_dynamic-update-slice_fusion, s32[]{:T(128)S(6)} %select_n.18), kind=kOutput, calls=%fused_computation.3 | convolution fusion | flops 12894339072 | bytes 29360132 | tf_op jit(solution)/shard_map/dot_general | solution.py:40
  306.4 25.8 %multiply_add_fusion = f32[2048,2048]{1,0:T(8,128)} fusion(f32[2048]{0:T(1024)S(1)} %bitcast.35, f32[2048]{0:T(1024)S(1)} %bitcast.34, bf16[2048,2048]{1,0:T(8,128)(2,1)} %fusion, f32[2048,768]{1,0:T(8,128)} %fusion.1, bf16[2048,2048]{1,0:T(8,128)(2,1)} %all-gather.4.cloned.1.call-done, bf16[2,768,2048]{2,1,0:T(8,128)(2,1)} %all-gather.8.cloned.1.call-done, ...), kind=kOutput, calls=%fused_computation | convolution fusion | flops 12919504896 | bytes 46153736 | tf_op jit(solution)/shard_map/dot_general | solution.py:40
  332.2 0.0 reduce-scatter.2.cloned.1.call-update
  332.2 168.3 %reduce-scatter.2.cloned.1.call-done = f32[256,2048]{1,0:T(8,128)} async-done(((f32[2048,2048]{1,0:T(8,128)}), f32[256,2048]{1,0:T(8,128)}) %reduce-scatter.2.cloned.1.call-update) | async-done | bytes 2097168 | tf_op jit(solution)/shard_map/reduce_scatter | solution.py:42
  500.5 2.7 convert_element_type.35
  (3 shorter events, 0.0 us)
Async XLA Ops:
  6.5 128.6 %copy-start.1 = (f32[256,8]{0,1:T(8,128)S(1)}, f32[256,8]{0,1:T(8,128)}, u32[]{:S(2)}) copy-start(f32[256,8]{0,1:T(8,128)} %param.10) | copy-start | bytes 24580
  6.5 128.6 %copy-start.2 = (s32[256,8]{0,1:T(8,128)S(1)}, s32[256,8]{0,1:T(8,128)}, u32[]{:S(2)}) copy-start(s32[256,8]{0,1:T(8,128)} %param.9) | copy-start | bytes 24580
  6.5 180.1 %all-gather.6.cloned.1.call-start = ((), (), s32[]{:S(2)}) async-start(), calls=%async_computation.3 | async-start | bytes 7864320 | tf_op jit(solution)/shard_map/all_gather | solution.py:28
  7.3 206.8 %all-gather.4.cloned.1.call-start = ((), (), s32[]{:S(2)}) async-start(), calls=%async_computation.2 | async-start | bytes 9437184 | tf_op jit(solution)/shard_map/all_gather | solution.py:19
  11.3 166.1 %copy-start = (bf16[2,512,768]{2,1,0:T(8,128)(2,1)S(1)}, bf16[2,512,768]{2,1,0:T(8,128)(2,1)}, u32[]{:S(2)}) copy-start(bf16[2,512,768]{2,1,0:T(8,128)(2,1)} %param.12) | copy-start | bytes 4718596
  11.4 272.9 %all-gather.8.cloned.1.call-start = ((), (), s32[]{:S(2)}) async-start(), calls=%async_computation.4 | async-start | bytes 7864320 | tf_op jit(solution)/shard_map/all_gather | solution.py:35
  11.4 58.0 %collective-permute-start = (bf16[2,512,768]{2,1,0:T(8,128)(2,1)}, bf16[2,512,768]{2,1,0:T(8,128)(2,1)S(1)}, u32[]{:S(2)}, u32[]{:S(2)}) collective-permute-start(bf16[2,512,768]{2,1,0:T(8,128)(2,1)} %param.12), channel_id=1, source_target_pairs={{0,8},{8,16},{16,24},{24,0},{1,9},{9,17},{17,25},{25,1},{2,10},{10... | collective-permute-start | bytes 4718600 | tf_op jit(solution)/shard_map/ppermute | solution.py:31
  69.4 64.9 %collective-permute-start.1 = (bf16[2,512,768]{2,1,0:T(8,128)(2,1)S(1)}, bf16[2,512,768]{2,1,0:T(8,128)(2,1)}, u32[]{:S(2)}, u32[]{:S(2)}) collective-permute-start(bf16[2,512,768]{2,1,0:T(8,128)(2,1)S(1)} %collective-permute-done), channel_id=1, source_target_pairs={{0,8},{8,16},{16,24},{24,0},{1,9},{9,17},{17,25},{25,1},{2,10},{10... | collective-permute-start | bytes 4718600 | tf_op jit(solution)/shard_map/ppermute | solution.py:31
  134.4 36.4 %collective-permute-start.2 = (bf16[2,512,768]{2,1,0:T(8,128)(2,1)}, bf16[2,512,768]{2,1,0:T(8,128)(2,1)}, u32[]{:S(2)}, u32[]{:S(2)}) collective-permute-start(bf16[2,512,768]{2,1,0:T(8,128)(2,1)} %collective-permute-done.1), channel_id=1, source_target_pairs={{0,8},{8,16},{16,24},{24,0},{1,9},{9,17},{17,25},{25,1},{2,10},{10... | collective-permute-start | bytes 4718600 | tf_op jit(solution)/shard_map/ppermute | solution.py:31
  135.8 12.0 %all-to-all-start = ((f32[256,8,2]{0,2,1:T(2,128)}), f32[256,8,2]{0,2,1:T(2,128)S(1)}, u32[]{:S(2)}, u32[]{:S(2)}) async-start(f32[256,8,2]{0,2,1:T(2,128)} %reshape.18), calls=%async_computation | async-start | bytes 32768 | tf_op jit(solution)/shard_map/all_to_all | solution.py:20
  140.7 359.8 %reduce-scatter.2.cloned.1.call-start = ((), (), s32[]{:S(2)}) async-start(), calls=%async_computation.5 | async-start | bytes 18874368 | tf_op jit(solution)/shard_map/reduce_scatter | solution.py:42
  214.1 11.8 %copy-start.3 = (bf16[2048,2048]{1,0:T(8,128)(2,1)S(1)}, bf16[2048,2048]{1,0:T(8,128)(2,1)}, u32[]{:S(2)}) copy-start(bf16[2048,2048]{1,0:T(8,128)(2,1)} %all-gather.4.cloned.1.call-done) | copy-start | bytes 25165828
  214.1 11.8 %copy-start.4 = (bf16[2,2048,768]{2,1,0:T(8,128)(2,1)S(1)}, bf16[2,2048,768]{2,1,0:T(8,128)(2,1)}, u32[]{:S(2)}) copy-start(bf16[2,2048,768]{2,1,0:T(8,128)(2,1)} %all-gather.6.cloned.1.call-done) | copy-start | bytes 18874372
Sparse Core Ops, SparseCore 0:
  9.2 120.6 all-gather.5
  131.5 82.5 all-gather.3
  215.9 68.2 all-gather.7
  332.3 168.1 reduce-scatter.1
